TPU v7x, 32 devices: a whole 2x2x4 slice. The times are simulated.
32 devices in a mesh: gx: 4 (over y, core), gy: 4 (over z), gz: 2 (over x).
Axes of the slice: x: 2, y: 2, z: 4, core: 2. Of those that a mesh axis runs over, the one named last changes fastest.
Arguments:
- grads: bfloat16 [32, 4, 1, 8, 3584], P(('gx', 'gy', 'gz')), may hold values from -1196032 to 1196032
- counts: int32 [32], P(('gx', 'gy', 'gz')), may hold values from 1 to 4
- total_tokens: int32 [1], replicated, may hold values from 4000000 to 15999999
- master: float32 [1, 8, 3584], P(None, 'gy', ('gx', 'gz')), may hold values from -6 to 6
- moment1: float32 [1, 8, 3584], P(None, 'gy', ('gx', 'gz')), may hold values from -2 to 2
- moment2: float32 [1, 8, 3584], P(None, 'gy', ('gx', 'gz')), may hold values from 0.01 to 1
Outputs:
- params: bfloat16 [1, 8, 3584], replicated
- master_out: float32 [1, 8, 3584], P(None, 'gy', ('gx', 'gz'))
- moment1_out: float32 [1, 8, 3584], P(None, 'gy', ('gx', 'gz'))
- moment2_out: float32 [1, 8, 3584], P(None, 'gy', ('gx', 'gz'))
All inputs are finite; a program needn't handle non-finite values.
Results may differ from a plain program's by a relative error of at most 0.0004.
Values may be sent and summed in bfloat16 or wider, within the bound.
A program may use at most 64 MiB of HBM per device.

v0:
```python
import jax
import jax.numpy as jnp
from jax import lax
from jax.sharding import PartitionSpec as P


def body(grads, counts, total_tokens, master, moment1, moment2):
    rank_grads = grads[0]
    slots = jnp.arange(rank_grads.shape[0], dtype=jnp.int32)
    weights = (slots < counts[0]).astype(jnp.float32)
    accumulated = jnp.zeros(rank_grads.shape[1:], jnp.float32)
    for slot in range(rank_grads.shape[0]):
        accumulated = accumulated + weights[slot] * rank_grads[slot].astype(jnp.float32)
    partial_value = lax.psum_scatter(accumulated, ("gx", "gz"), scatter_dimension=2, tiled=True)
    summed = lax.psum_scatter(partial_value, "gy", scatter_dimension=1, tiled=True)
    gradient = summed / total_tokens.astype(jnp.float32)[0]
    moment1_out = 0.9 * moment1 + 0.1 * gradient
    moment2_out = 0.95 * moment2 + 0.05 * gradient * gradient
    first_fix = 1.0 - 0.9**10
    second_fix = 1.0 - 0.95**10
    update = moment1_out / first_fix / (jnp.sqrt(moment2_out / second_fix) + 1e-08)
    master_out = master - 0.01 * (update + 0.1 * master)
    shard_params = master_out.astype(jnp.bfloat16)
    wide_params = lax.all_gather(shard_params, ("gx", "gz"), axis=2, tiled=True)
    params = lax.all_gather(wide_params, "gy", axis=1, tiled=True)
    return (params, master_out, moment1_out, moment2_out)


def solution(mesh):
    return jax.shard_map(
        body,
        mesh=mesh,
        in_specs=(
            P(("gx", "gy", "gz"), None, None, None, None),
            P(("gx", "gy", "gz")),
            P(),
            P(None, "gy", ("gx", "gz")),
            P(None, "gy", ("gx", "gz")),
            P(None, "gy", ("gx", "gz")),
        ),
        out_specs=(
            P(),
            P(None, "gy", ("gx", "gz")),
            P(None, "gy", ("gx", "gz")),
            P(None, "gy", ("gx", "gz")),
        ),
        check_vma=False,
    )
```

profile of v0, /device:TPU:0, one launch (start us, length us, event | category | flops | bytes accessed | tf_op | source)
XLA Modules:
  0.0 125.8 jit_solution(12063351168490614243)
XLA Ops:
  7.2 0.0 reduce-scatter.5.cloned.1.call-start
  7.9 0.6 fusion.3
  8.5 3.5 %add_bitcast_fusion = f32[1,8,3584]{2,1,0:T(8,128)S(1)} fusion(bf16[1,4,1,8,3584]{4,3,2,1,0:T(8,128)(2,1)} %param.6, f32[]{:T(128)} %bitcast.8, f32[]{:T(128)} %bitcast.7, f32[]{:T(128)} %bitcast.6, f32[]{:T(128)} %bitcast.5), kind=kLoop, calls=%fused_computation | loop fusion | flops 315392 | bytes 344080 | tf_op jit(solution)/shard_map/add | solution.py:13
  12.0 0.0 copy-start.3
  12.0 0.0 copy-start
  12.0 0.0 copy-start.1
  12.0 0.0 copy-start.2
  12.0 3.0 %copy.13 = f32[1,8,3584]{1,0,2:T(1,128)} copy(f32[1,8,3584]{2,1,0:T(8,128)S(1)} %add_bitcast_fusion) | data formatting | bytes 229376
  15.0 0.0 reduce-scatter.5.cloned.1.call-update
  15.7 0.0 copy-done.3
  15.7 0.6 dynamic-slice
  17.0 40.5 %reduce-scatter.5.cloned.1.call-done = f32[448,8]{1,0:T(8,128)} async-done(((f32[3584,8]{1,0:T(8,128)}), f32[448,8]{1,0:T(8,128)}) %reduce-scatter.5.cloned.1.call-update) | async-done | bytes 14352
  57.5 1.0 copy.14
  58.5 18.7 %all-reduce = f32[1,8,448]{2,1,0:T(8,128)S(1)} all-reduce(f32[1,8,448]{2,1,0:T(8,128)S(1)} %copy.14), channel_id=3, replica_groups=mesh['gx'=4,'gy'=4,'gz'=2] {'gy'}, use_global_device_ids=true, to_apply=%region_1.0.clone | all-reduce | flops 3584 | bytes 28672
  77.2 0.0 copy-done
  77.2 0.0 copy-done.1
  77.2 0.0 copy-done.2
  77.3 0.6 fusion.1
  77.9 0.2 copy.10
  78.1 24.8 %all_gather.6 = bf16[1,2,3584]{1,0,2:T(2,128)(2,1)S(1)} all-gather(bf16[1,2,448]{1,0,2:T(2,128)(2,1)S(1)} %copy.10), channel_id=1, replica_groups=mesh['gx'=4,'gy'=4,'gz'=2] {'gx','gz'}, dimensions={2}, use_global_device_ids=true | all-gather | bytes 16128 | tf_op jit(solution)/shard_map/all_gather | solution.py:24
  102.9 2.0 %copy.11 = bf16[1,2,3584]{2,0,1:T(2,128)(2,1)S(1)} copy(bf16[1,2,3584]{1,0,2:T(2,128)(2,1)S(1)} %all_gather.6) | data formatting | bytes 28672 | tf_op jit(solution)/shard_map/all_gather | solution.py:24
  104.9 13.4 %all_gather.7 = bf16[1,8,3584]{2,0,1:T(2,128)(2,1)S(1)} all-gather(bf16[1,2,3584]{2,0,1:T(2,128)(2,1)S(1)} %copy.11), channel_id=1, replica_groups=mesh['gx'=4,'gy'=4,'gz'=2] {'gy'}, dimensions={1}, use_global_device_ids=true | all-gather | bytes 71680 | tf_op jit(solution)/shard_map/all_gather | solution.py:25
  118.3 0.6 copy.12
  (1 shorter events, 0.0 us)
Async XLA Ops:
  7.2 50.3 %reduce-scatter.5.cloned.1.call-start = ((), (), s32[]{:S(2)}) async-start(), calls=%async_computation.1 | async-start | bytes 2064384
  12.0 3.7 %copy-start.3 = (u32[32]{0:T(128)S(1)}, u32[32]{0:T(128)}, u32[]{:S(2)}) copy-start(u32[32]{0:T(128)} %constant.25) | copy-start | bytes 388
  12.0 65.2 %copy-start = (f32[1,2,448]{2,1,0:T(2,128)S(1)}, f32[1,2,448]{2,1,0:T(2,128)}, u32[]{:S(2)}) copy-start(f32[1,2,448]{2,1,0:T(2,128)} %param.9) | copy-start | bytes 10756
  12.0 65.2 %copy-start.1 = (f32[1,2,448]{2,1,0:T(2,128)S(1)}, f32[1,2,448]{2,1,0:T(2,128)}, u32[]{:S(2)}) copy-start(f32[1,2,448]{2,1,0:T(2,128)} %param.10) | copy-start | bytes 10756
  12.0 65.2 %copy-start.2 = (f32[1,2,448]{2,1,0:T(2,128)S(1)}, f32[1,2,448]{2,1,0:T(2,128)}, u32[]{:S(2)}) copy-start(f32[1,2,448]{2,1,0:T(2,128)} %param.11) | copy-start | bytes 10756
Sparse Core Ops, SparseCore 0:
  15.2 42.2 reduce-scatter.4
where the time goes:
time: 126 us
  blocking collectives  57 us (45%)
  waiting for transfers between devices  40.5 us (32%)
  between operations  16.1 us (13%)
  local copies, waits for them, and re-layouts  8.05 us (6%)
  other arithmetic  4.17 us (3%)
    unnamed x2, waiting for transfers between devices  40.5 us
    all_gather x1, blocking collectives, body(): wide_params = lax.all_gather(shard_params, ('gx', 'gz'), axis=2, tiled=True)  24.8 us
    unnamed x1, blocking collectives  18.7 us
    all_gather x1, blocking collectives, body(): params = lax.all_gather(wide_params, 'gy', axis=1, tiled=True)  13.4 us
    unnamed x12, local copies, waits for them, and re-layouts  5.27 us
    add x1, other arithmetic, body(): accumulated + weights[slot] * rank_grads[slot].astype(jnp.float32)  3.53 us
  transfers between devices with their start and end apart: 1, of which 1 were waited for; matrix products, arithmetic and copies ran while one was open for 0% of the time, Pallas kernels for 0%

commit v1 on v0

v1 whole, which is shorter than its diff:
```python
import functools

import jax
import jax.numpy as jnp
from jax import lax
from jax.experimental import pallas as pl
from jax.experimental.pallas import tpu as pltpu
from jax.sharding import PartitionSpec as P

MESH = pl.DeviceIdType.MESH
LANES = 128


class Cut:
    def __init__(self, width, blocks):
        self.width, self.blocks = width, blocks
        self.own = width // blocks
        tiles = max(-(-(c + 1) * self.own // LANES) - c * self.own // LANES for c in range(blocks))
        self.window = tiles * LANES
        self.last = width // LANES - tiles
        self.offsets = sorted({self.offset(c) for c in range(blocks)})

    def tile(self, c):
        if isinstance(c, int):
            return min(c * self.own // LANES, self.last)
        return jnp.minimum(lax.div(c * self.own, LANES), self.last)

    def offset(self, c):
        return c * self.own - LANES * self.tile(c)

    def into(self, x, offset):
        rows = x.shape[0]
        result = None
        for o in self.offsets:
            parts = [jnp.zeros((rows, o), x.dtype)] if o else []
            parts.append(x)
            rest = self.window - o - self.own
            if rest:
                parts.append(jnp.zeros((rows, rest), x.dtype))
            moved = jnp.concatenate(parts, axis=1) if len(parts) > 1 else x
            result = moved if result is None else jnp.where(offset == o, moved, result)
        return result

    def out_of(self, x, offset):
        result = None
        for o in self.offsets:
            moved = x[:, o : o + self.own]
            result = moved if result is None else jnp.where(offset == o, moved, result)
        return result


def each_peer(sizes, me, visit):
    nx, ny, nz = sizes
    gx, gy, gz = me
    if nx * ny * nz <= 64:
        xs = [gx] + [lax.rem(gx + a, nx) for a in range(1, nx)]
        ys = [gy] + [lax.rem(gy + b, ny) for b in range(1, ny)]
        zs = [gz] + [lax.rem(gz + c, nz) for c in range(1, nz)]
        order = sorted(range(ny), key=lambda b: -min(b, ny - b))
        for b in order:
            for a in range(nx):
                for c in range(nz):
                    slot = (b * nx + a) * nz + c - 1
                    if slot >= 0:
                        visit(slot, (xs[a], ys[b], zs[c]))
    else:

        def step(k, carry):
            c = lax.rem(k, nz)
            a = lax.rem(lax.div(k, nz), nx)
            b = lax.div(k, nz * nx)
            visit(k - 1, (lax.rem(gx + a, nx), lax.rem(gy + b, ny), lax.rem(gz + c, nz)))
            return carry

        lax.fori_loop(1, nx * ny * nz, step, 0)


def kernel(
    sizes,
    cut,
    grads,
    counts,
    tokens,
    master,
    moment1,
    moment2,
    params_out,
    master_out,
    moment1_out,
    moment2_out,
    grad_buf,
    state_buf,
    count_buf,
    token_buf,
    stage,
    recv,
    shard,
    gathered,
    local_sem,
    rs_send,
    rs_recv,
    ag_send,
    ag_recv,
):
    nx, ny, nz = sizes
    n = nx * ny * nz
    gx, gy, gz = me = (lax.axis_index("gx"), lax.axis_index("gy"), lax.axis_index("gz"))
    rows = stage.shape[1]
    window = cut.window

    loads = [
        pltpu.make_async_copy(grads, grad_buf, local_sem.at[0]),
        pltpu.make_async_copy(counts, count_buf, local_sem.at[1]),
        pltpu.make_async_copy(tokens, token_buf, local_sem.at[2]),
        pltpu.make_async_copy(master, state_buf.at[0], local_sem.at[3]),
        pltpu.make_async_copy(moment1, state_buf.at[1], local_sem.at[4]),
        pltpu.make_async_copy(moment2, state_buf.at[2], local_sem.at[5]),
    ]
    for load in loads:
        load.start()

    barrier = pltpu.get_barrier_semaphore()
    each_peer(
        sizes,
        me,
        lambda slot, peer: pl.semaphore_signal(barrier, inc=1, device_id=peer, device_id_type=MESH),
    )

    loads[1].wait()
    loads[0].wait()
    count = count_buf[0]
    total = None
    for m in range(grad_buf.shape[0]):
        weight = jnp.where(m < count, jnp.float32(1.0), jnp.float32(0.0))
        term = weight * grad_buf[m].astype(jnp.float32)
        total = term if total is None else total + term
    for g in range(ny):
        stage[g] = total[g * rows : (g + 1) * rows]

    pl.semaphore_wait(barrier, n - 1)

    def send_sum(slot, peer):
        start = pl.multiple_of(LANES * cut.tile(peer[0] * nz + peer[2]), LANES)
        pltpu.make_async_remote_copy(
            src_ref=stage.at[peer[1], :, pl.ds(start, window)],
            dst_ref=recv.at[slot],
            send_sem=rs_send,
            recv_sem=rs_recv,
            device_id=peer,
            device_id_type=MESH,
        ).start()

    each_peer(sizes, me, send_sum)

    column = gx * nz + gz
    offset = cut.offset(column)
    for load in loads[2:]:
        load.wait()
    old_master = cut.into(state_buf[0], offset)
    old_moment1 = cut.into(state_buf[1], offset)
    old_moment2 = cut.into(state_buf[2], offset)
    scale = token_buf[0].astype(jnp.float32)
    start = pl.multiple_of(LANES * cut.tile(column), LANES)
    own = stage[gy, :, pl.ds(start, window)]

    pltpu.make_async_copy(recv, recv, rs_recv).wait()
    if n <= 64:
        terms = [own] + [recv[k] for k in range(n - 1)]
        while len(terms) > 1:
            terms = [a + b for a, b in zip(terms[::2], terms[1::2])] + terms[len(terms) - len(terms) % 2 :]
        summed = terms[0]
    else:
        summed = lax.fori_loop(0, n - 1, lambda k, s: s + recv[k], own)
    gradient = summed / scale
    new_moment1 = 0.9 * old_moment1 + 0.1 * gradient
    new_moment2 = 0.95 * old_moment2 + 0.05 * gradient * gradient
    first_fix = 1.0 - 0.9**10
    second_fix = 1.0 - 0.95**10
    update = new_moment1 / first_fix / (jnp.sqrt(new_moment2 / second_fix) + 1e-08)
    new_master = old_master - 0.01 * (update + 0.1 * old_master)
    new_params = new_master.astype(jnp.bfloat16)
    shard[...] = new_params

    mine = gy * (nx * nz) + column

    def send_params(slot, peer):
        pltpu.make_async_remote_copy(
            src_ref=shard,
            dst_ref=gathered.at[mine],
            send_sem=ag_send,
            recv_sem=ag_recv,
            device_id=peer,
            device_id_type=MESH,
        ).start()

    each_peer(sizes, me, send_params)

    gathered[mine] = new_params
    master_out[...] = cut.out_of(new_master, offset)
    moment1_out[...] = cut.out_of(new_moment1, offset)
    moment2_out[...] = cut.out_of(new_moment2, offset)
    pltpu.make_async_copy(recv, recv, rs_send).wait()
    others = gathered.at[pl.ds(0, n - 1)]
    pltpu.make_async_copy(others, others, ag_send).wait()
    pltpu.make_async_copy(others, others, ag_recv).wait()

    lane = lax.broadcasted_iota(jnp.int32, (rows, LANES), 1)
    for g in range(ny):
        tiles = []
        for t in range(cut.width // LANES):
            value = None
            for c in range(cut.blocks):
                first = c * cut.own - t * LANES
                if first + cut.own <= 0 or first >= LANES:
                    continue
                at = (t - cut.tile(c)) * LANES
                piece = gathered[g * cut.blocks + c, :, at : at + LANES]
                value = piece if value is None else jnp.where(lane >= first, piece, value)
            tiles.append(value)
        params_out[g * rows : (g + 1) * rows, :] = jnp.concatenate(tiles, axis=1)


def solution(mesh):
    sizes = tuple(mesh.shape[axis] for axis in ("gx", "gy", "gz"))
    nx, ny, nz = sizes
    n = nx * ny * nz

    def body(grads, counts, total_tokens, master, moment1, moment2):
        micro, _, all_rows, width = grads.shape[1:]
        rows, own = master.shape[1:]
        cut = Cut(width, nx * nz)
        anywhere = pl.BlockSpec(memory_space=pl.ANY)
        vmem = pl.BlockSpec(memory_space=pltpu.VMEM)
        part = jax.ShapeDtypeStruct((rows, own), jnp.float32)
        params, *state = pl.pallas_call(
            functools.partial(kernel, sizes, cut),
            out_shape=[jax.ShapeDtypeStruct((all_rows, width), jnp.bfloat16), part, part, part],
            in_specs=[anywhere] * 6,
            out_specs=[vmem] * 4,
            scratch_shapes=[
                pltpu.VMEM((micro, all_rows, width), jnp.bfloat16),
                pltpu.VMEM((3, rows, own), jnp.float32),
                pltpu.SMEM((1,), jnp.int32),
                pltpu.SMEM((1,), jnp.int32),
                pltpu.VMEM((ny, rows, width), jnp.float32),
                pltpu.VMEM((n - 1, rows, cut.window), jnp.float32),
                pltpu.VMEM((rows, cut.window), jnp.bfloat16),
                pltpu.VMEM((n, rows, cut.window), jnp.bfloat16),
                pltpu.SemaphoreType.DMA((6,)),
                pltpu.SemaphoreType.DMA,
                pltpu.SemaphoreType.DMA,
                pltpu.SemaphoreType.DMA,
                pltpu.SemaphoreType.DMA,
            ],
            compiler_params=pltpu.CompilerParams(collective_id=0, has_side_effects=True),
            name="step",
        )(
            grads.reshape(micro, all_rows, width),
            counts,
            total_tokens,
            master.reshape(rows, own),
            moment1.reshape(rows, own),
            moment2.reshape(rows, own),
        )
        return (params[None], *(array[None] for array in state))

    sharded = P(None, "gy", ("gx", "gz"))
    return jax.shard_map(
        body,
        mesh=mesh,
        in_specs=(P(("gx", "gy", "gz"), None, None, None, None), P(("gx", "gy", "gz")), P(), sharded, sharded, sharded),
        out_specs=(P(), sharded, sharded, sharded),
        check_vma=False,
    )
```

time: 126 us -> 24 us (0.19)
  blocking collectives: 57 us -> 0 us
  waiting for transfers between devices: 40.5 us -> 0 us
  Pallas kernels: 0 us -> 18.4 us
  between operations: 16.1 us -> 1.94 us
  local copies, waits for them, and re-layouts: 8.05 us -> 3.4 us
  other arithmetic: 4.17 us -> 0 us
    unnamed x2 -> x0, waiting for transfers between devices: 40.5 us -> none
    all_gather x2 -> x0, blocking collectives: 38.2 us -> none  [the longest x1 24.8 us: body(): wide_params = lax.all_gather(shard_params, ('gx', 'gz'), axis=2, tiled=True)]
    unnamed x1 -> x0, blocking collectives: 18.7 us -> none
    pallas_call x0 -> x1, Pallas kernels: none -> 18.4 us  [body(): pl.pallas_call(functools.partial(kernel, sizes, cut), out_shape=[jax.Shap...]
    add x1 -> x0, other arithmetic: 3.53 us -> none  [body(): accumulated + weights[slot] * rank_grads[slot].astype(jnp.float32)]
    all_gather x1 -> x0, local copies, waits for them, and re-layouts: 1.99 us -> none  [body(): wide_params = lax.all_gather(shard_params, ('gx', 'gz'), axis=2, tiled=True)]
    unnamed x12 -> x10, local copies, waits for them, and re-layouts: 5.27 us -> 3.4 us
  transfers between devices with their start and end apart: 1 -> 0, of which waited for: 1 -> 0; matrix products, arithmetic and copies ran while one was open for 0% -> 0% of each run, Pallas kernels for 0% -> 0%
where the time goes in v1:
time: 24 us; the launch traced here: 23.7 us
  Pallas kernels  18.4 us (77%)
  local copies, waits for them, and re-layouts  3.4 us (14%)
  between operations  1.94 us (8%)
    pallas_call x1, Pallas kernels, body(): pl.pallas_call(functools.partial(kernel, sizes, cut), out_shape=[jax.Shap...  18.4 us
    unnamed x10, local copies, waits for them, and re-layouts  3.4 us

profile of v1, /device:TPU:0, one launch (start us, length us, event | category | flops | bytes accessed | tf_op | source)
XLA Modules:
  0.0 23.7 jit_solution(2029727549653291728)
XLA Ops:
  1.9 18.4 %step.1 = (bf16[8,3584]{1,0:T(8,128)(2,1)}, f32[2,448]{1,0:T(2,128)}, f32[2,448]{1,0:T(2,128)}, f32[2,448]{1,0:T(2,128)}) custom-call(bf16[4,8,3584]{2,1,0:T(8,128)(2,1)} %bitcast.8, s32[1]{0:T(128)S(6)} %copy.14.counts, s32[1]{0:T(128)S(6)} %copy.15.tokens, f32[2,448]{1,0:T(2,128)} %bitcast.10, f32[2,448]{1,0:T(2,128)} %bitcast.11, f32[2,448]{1,0:T(2,128)} %bitcast.12), custom_call_target="tpu_custom_call" | custom-call | tf_op jit(solution)/shard_map/step/pallas_call | solution.py:235
  20.3 0.0 copy-start.2
  20.3 1.4 %copy.16 = bf16[1,8,3584]{2,1,0:T(8,128)(2,1)} copy(bf16[1,8,3584]{2,1,0:T(8,128)(2,1)} %bitcast.9) | data formatting | bytes 114688
  21.8 0.0 copy-done.2
  21.8 0.0 copy-start.1
  21.8 0.6 %copy.17 = f32[1,2,448]{2,1,0:T(2,128)} copy(f32[1,2,448]{2,1,0:T(2,128)S(1)} %bitcast.15) | data formatting | bytes 7168
  22.4 0.1 copy-done.1
  22.4 0.0 copy-start
  22.4 0.6 %copy.18 = f32[1,2,448]{2,1,0:T(2,128)} copy(f32[1,2,448]{2,1,0:T(2,128)S(1)} %bitcast.14) | data formatting | bytes 7168
  23.0 0.1 copy-done
  23.1 0.6 %copy.19 = f32[1,2,448]{2,1,0:T(2,128)} copy(f32[1,2,448]{2,1,0:T(2,128)S(1)} %bitcast.13) | data formatting | bytes 7168
Async XLA Ops:
  20.3 1.5 %copy-start.2 = (f32[2,448]{1,0:T(2,128)S(1)}, f32[2,448]{1,0:T(2,128)}, u32[]{:S(2)}) copy-start(f32[2,448]{1,0:T(2,128)} %get-tuple-element.9) | copy-start | bytes 10756
  21.8 0.7 %copy-start.1 = (f32[2,448]{1,0:T(2,128)S(1)}, f32[2,448]{1,0:T(2,128)}, u32[]{:S(2)}) copy-start(f32[2,448]{1,0:T(2,128)} %get-tuple-element.10) | copy-start | bytes 10756
  22.4 0.7 %copy-start = (f32[2,448]{1,0:T(2,128)S(1)}, f32[2,448]{1,0:T(2,128)}, u32[]{:S(2)}) copy-start(f32[2,448]{1,0:T(2,128)} %get-tuple-element.11) | copy-start | bytes 10756

commit v2 on v1

--- a/solution.py
+++ b/solution.py
@@ -84,18 +84,13 @@
     master,
     moment1,
     moment2,
-    params_out,
-    master_out,
-    moment1_out,
-    moment2_out,
+    gathered,
+    state,
     grad_buf,
     state_buf,
-    count_buf,
-    token_buf,
     stage,
     recv,
     shard,
-    gathered,
     local_sem,
     rs_send,
     rs_recv,
@@ -110,8 +105,6 @@
 
     loads = [
         pltpu.make_async_copy(grads, grad_buf, local_sem.at[0]),
-        pltpu.make_async_copy(counts, count_buf, local_sem.at[1]),
-        pltpu.make_async_copy(tokens, token_buf, local_sem.at[2]),
         pltpu.make_async_copy(master, state_buf.at[0], local_sem.at[3]),
         pltpu.make_async_copy(moment1, state_buf.at[1], local_sem.at[4]),
         pltpu.make_async_copy(moment2, state_buf.at[2], local_sem.at[5]),
@@ -126,9 +119,8 @@
         lambda slot, peer: pl.semaphore_signal(barrier, inc=1, device_id=peer, device_id_type=MESH),
     )
 
-    loads[1].wait()
     loads[0].wait()
-    count = count_buf[0]
+    count = counts[0]
     total = None
     for m in range(grad_buf.shape[0]):
         weight = jnp.where(m < count, jnp.float32(1.0), jnp.float32(0.0))
@@ -154,12 +146,12 @@
 
     column = gx * nz + gz
     offset = cut.offset(column)
-    for load in loads[2:]:
+    for load in loads[1:]:
         load.wait()
     old_master = cut.into(state_buf[0], offset)
     old_moment1 = cut.into(state_buf[1], offset)
     old_moment2 = cut.into(state_buf[2], offset)
-    scale = token_buf[0].astype(jnp.float32)
+    scale = tokens[0].astype(jnp.float32)
     start = pl.multiple_of(LANES * cut.tile(column), LANES)
     own = stage[gy, :, pl.ds(start, window)]
 
@@ -196,13 +188,26 @@
     each_peer(sizes, me, send_params)
 
     gathered[mine] = new_params
-    master_out[...] = cut.out_of(new_master, offset)
-    moment1_out[...] = cut.out_of(new_moment1, offset)
-    moment2_out[...] = cut.out_of(new_moment2, offset)
+    state[0] = new_master
+    state[1] = new_moment1
+    state[2] = new_moment2
     pltpu.make_async_copy(recv, recv, rs_send).wait()
     others = gathered.at[pl.ds(0, n - 1)]
     pltpu.make_async_copy(others, others, ag_send).wait()
     pltpu.make_async_copy(others, others, ag_recv).wait()
+
+
+def finish(
+    sizes, cut, gathered, state, params_out, master_out, moment1_out, moment2_out, params_buf, state_buf, sem
+):
+    nx, ny, nz = sizes
+    rows = gathered.shape[1]
+    offset = cut.offset(lax.axis_index("gx") * nz + lax.axis_index("gz"))
+    copies = []
+    for k, out in enumerate((master_out, moment1_out, moment2_out)):
+        state_buf[k] = cut.out_of(state[k], offset)
+        copies.append(pltpu.make_async_copy(state_buf.at[k], out, sem.at[k]))
+        copies[-1].start()
 
     lane = lax.broadcasted_iota(jnp.int32, (rows, LANES), 1)
     for g in range(ny):
@@ -217,7 +222,11 @@
                 piece = gathered[g * cut.blocks + c, :, at : at + LANES]
                 value = piece if value is None else jnp.where(lane >= first, piece, value)
             tiles.append(value)
-        params_out[g * rows : (g + 1) * rows, :] = jnp.concatenate(tiles, axis=1)
+        params_buf[g * rows : (g + 1) * rows, :] = jnp.concatenate(tiles, axis=1)
+    copies.append(pltpu.make_async_copy(params_buf, params_out, sem.at[3]))
+    copies[-1].start()
+    for copy in copies:
+        copy.wait()
 
 
 def solution(mesh):
@@ -229,23 +238,24 @@
         micro, _, all_rows, width = grads.shape[1:]
         rows, own = master.shape[1:]
         cut = Cut(width, nx * nz)
-        anywhere = pl.BlockSpec(memory_space=pl.ANY)
+        hbm = pl.BlockSpec(memory_space=pltpu.HBM)
         vmem = pl.BlockSpec(memory_space=pltpu.VMEM)
+        scalar = pl.BlockSpec(memory_space=pltpu.SMEM)
         part = jax.ShapeDtypeStruct((rows, own), jnp.float32)
-        params, *state = pl.pallas_call(
+        gathered, state = pl.pallas_call(
             functools.partial(kernel, sizes, cut),
-            out_shape=[jax.ShapeDtypeStruct((all_rows, width), jnp.bfloat16), part, part, part],
-            in_specs=[anywhere] * 6,
-            out_specs=[vmem] * 4,
+            out_shape=[
+                pltpu.VMEM((n, rows, cut.window), jnp.bfloat16),
+                pltpu.VMEM((3, rows, cut.window), jnp.float32),
+            ],
+            in_specs=[hbm, scalar, scalar, hbm, hbm, hbm],
+            out_specs=[vmem] * 2,
             scratch_shapes=[
                 pltpu.VMEM((micro, all_rows, width), jnp.bfloat16),
                 pltpu.VMEM((3, rows, own), jnp.float32),
-                pltpu.SMEM((1,), jnp.int32),
-                pltpu.SMEM((1,), jnp.int32),
                 pltpu.VMEM((ny, rows, width), jnp.float32),
                 pltpu.VMEM((n - 1, rows, cut.window), jnp.float32),
                 pltpu.VMEM((rows, cut.window), jnp.bfloat16),
-                pltpu.VMEM((n, rows, cut.window), jnp.bfloat16),
                 pltpu.SemaphoreType.DMA((6,)),
                 pltpu.SemaphoreType.DMA,
                 pltpu.SemaphoreType.DMA,
@@ -262,7 +272,22 @@
             moment1.reshape(rows, own),
             moment2.reshape(rows, own),
         )
-        return (params[None], *(array[None] for array in state))
+        params, *parts = pl.pallas_call(
+            functools.partial(finish, sizes, cut),
+            out_shape=[jax.ShapeDtypeStruct((all_rows, width), jnp.bfloat16), part, part, part],
+            in_specs=[vmem] * 2,
+            out_specs=[hbm] * 4,
+            scratch_shapes=[
+                pltpu.VMEM((all_rows, width), jnp.bfloat16),
+                pltpu.VMEM((3, rows, own), jnp.float32),
+                pltpu.SemaphoreType.DMA((4,)),
+            ],
+            name="finish",
+        )(
+            pltpu.with_memory_space_constraint(gathered, pltpu.VMEM),
+            pltpu.with_memory_space_constraint(state, pltpu.VMEM),
+        )
+        return (params[None], *(array[None] for array in parts))
 
     sharded = P(None, "gy", ("gx", "gz"))
     return jax.shard_map(

time: 24 us -> 20.6 us (0.86)
  local copies, waits for them, and re-layouts: 3.4 us -> 0 us
    unnamed x10 -> x0, local copies, waits for them, and re-layouts: 3.4 us -> none
    pallas_call x1 -> x2, Pallas kernels: 18.4 us -> 18.5 us  [the longest x1 17.7 us: body(): pl.pallas_call(functools.partial(kernel, sizes, cut), out_shape=[pltpu.VM...]
where the time goes in v2:
time: 20.6 us; the launch traced here: 20.4 us
  Pallas kernels  18.5 us (90%)
  between operations  1.93 us (9%)
    pallas_call x1, Pallas kernels, body(): pl.pallas_call(functools.partial(kernel, sizes, cut), out_shape=[pltpu.VM...  17.7 us
    pallas_call x1, Pallas kernels, body(): pl.pallas_call(functools.partial(finish, sizes, cut), out_shape=[jax.Shap...  0.81 us

profile of v2, /device:TPU:0, one launch (start us, length us, event | category | flops | bytes accessed | tf_op | source)
XLA Modules:
  0.0 20.4 jit_solution(13511298125671145813)
XLA Ops:
  1.9 17.7 %step.1 = (bf16[32,2,512]{2,1,0:T(2,128)(2,1)S(1)}, f32[3,2,512]{2,1,0:T(2,128)S(1)}) custom-call(bf16[4,8,3584]{2,1,0:T(8,128)(2,1)} %bitcast.8, s32[1]{0:T(128)S(6)} %copy.10.counts, s32[1]{0:T(128)S(6)} %copy.11.tokens, f32[2,448]{1,0:T(2,128)} %bitcast.9, f32[2,448]{1,0:T(2,128)} %bitcast.10, f32[2,448]{1,0:T(2,128)} %bitcast.11), custom_call_target="tpu_custom_call" | custom-call | tf_op jit(solution)/shard_map/step/pallas_call | solution.py:245
  19.6 0.8 %finish.1 = (bf16[8,3584]{1,0:T(8,128)(2,1)}, f32[2,448]{1,0:T(2,128)}, f32[2,448]{1,0:T(2,128)}, f32[2,448]{1,0:T(2,128)}) custom-call(bf16[32,2,512]{2,1,0:T(2,128)(2,1)S(1)} %get-tuple-element.10.gathered, f32[3,2,512]{2,1,0:T(2,128)S(1)} %get-tuple-element.11.state), custom_call_target="tpu_custom_call" | custom-call | tf_op jit(solution)/shard_map/finish/pallas_call | solution.py:275

commit v3 on v2

v3 whole, which is shorter than its diff:
```python
import functools

import jax
import jax.numpy as jnp
from jax import lax
from jax.experimental import pallas as pl
from jax.experimental.pallas import tpu as pltpu
from jax.sharding import PartitionSpec as P

MESH = pl.DeviceIdType.MESH
LANES = 128


class Cut:
    def __init__(self, width, blocks):
        self.width, self.blocks = width, blocks
        self.own = width // blocks
        tiles = max(-(-(c + 1) * self.own // LANES) - c * self.own // LANES for c in range(blocks))
        self.window = tiles * LANES
        self.last = width // LANES - tiles
        self.offsets = sorted({self.offset(c) for c in range(blocks)})

    def tile(self, c):
        if isinstance(c, int):
            return min(c * self.own // LANES, self.last)
        return jnp.minimum(lax.div(c * self.own, LANES), self.last)

    def offset(self, c):
        return c * self.own - LANES * self.tile(c)

    def into(self, x, offset):
        rows = x.shape[0]
        result = None
        for o in self.offsets:
            parts = [jnp.zeros((rows, o), x.dtype)] if o else []
            parts.append(x)
            rest = self.window - o - self.own
            if rest:
                parts.append(jnp.zeros((rows, rest), x.dtype))
            moved = jnp.concatenate(parts, axis=1) if len(parts) > 1 else x
            result = moved if result is None else jnp.where(offset == o, moved, result)
        return result

    def out_of(self, x, offset):
        result = None
        for o in self.offsets:
            moved = x[:, o : o + self.own]
            result = moved if result is None else jnp.where(offset == o, moved, result)
        return result


def plane_peers(sizes, me):
    nx, ny, nz = sizes
    gx, gy, gz = me
    xs = [gx] + [lax.rem(gx + a, nx) for a in range(1, nx)]
    zs = [gz] + [lax.rem(gz + c, nz) for c in range(1, nz)]
    order = sorted(range(1, nx * nz), key=lambda k: (-min(k % nz, nz - k % nz), -min(k // nz, nx - k // nz)))
    return [(k - 1, (xs[k // nz], gy, zs[k % nz])) for k in order]


def line_peers(sizes, me):
    nx, ny, nz = sizes
    gx, gy, gz = me
    return [(gx, lax.rem(gy + b, ny), gz) for b in sorted(range(1, ny), key=lambda b: -min(b, ny - b))]


def send(src, dst, sems, k, peer):
    copy = pltpu.make_async_remote_copy(
        src_ref=src,
        dst_ref=dst,
        send_sem=sems.at[0, k],
        recv_sem=sems.at[1, k],
        device_id=peer,
        device_id_type=MESH,
    )
    copy.start()


def wait_all(ref, sem):
    pltpu.make_async_copy(ref, ref, sem).wait()


def tree_sum(terms):
    while len(terms) > 1:
        terms = [a + b for a, b in zip(terms[::2], terms[1::2])] + terms[len(terms) - len(terms) % 2 :]
    return terms[0]


def kernel(
    sizes,
    cut,
    grads,
    counts,
    tokens,
    master,
    moment1,
    moment2,
    gathered,
    state,
    grad_buf,
    lines,
    stage,
    recv,
    planes,
    shard,
    local_sem,
    sems,
):
    nx, ny, nz = sizes
    gx, gy, gz = me = (lax.axis_index("gx"), lax.axis_index("gy"), lax.axis_index("gz"))
    plane, line = plane_peers(sizes, me), line_peers(sizes, me)
    window = cut.window

    loads = [
        pltpu.make_async_copy(grads, grad_buf, local_sem.at[0]),
        pltpu.make_async_copy(master, lines.at[gy, 0], local_sem.at[1]),
        pltpu.make_async_copy(moment1, lines.at[gy, 1], local_sem.at[2]),
        pltpu.make_async_copy(moment2, lines.at[gy, 2], local_sem.at[3]),
    ]
    for load in loads:
        load.start()

    barrier = pltpu.get_barrier_semaphore()
    for peer in line + [peer for _, peer in plane]:
        pl.semaphore_signal(barrier, inc=1, device_id=peer, device_id_type=MESH)

    loads[0].wait()
    count = counts[0]
    total = None
    for m in range(grad_buf.shape[0]):
        weight = jnp.where(m < count, jnp.float32(1.0), jnp.float32(0.0))
        term = weight * grad_buf[m].astype(jnp.float32)
        total = term if total is None else total + term
    stage[...] = total

    pl.semaphore_wait(barrier, len(line) + len(plane))

    for slot, peer in plane:
        start = pl.multiple_of(LANES * cut.tile(peer[0] * nz + peer[2]), LANES)
        send(stage.at[:, pl.ds(start, window)], recv.at[slot], sems, 0, peer)
    for load in loads[1:]:
        load.wait()
    for peer in line:
        send(lines.at[gy], lines.at[gy], sems, 1, peer)

    column = gx * nz + gz
    offset = cut.offset(column)
    scale = tokens[0].astype(jnp.float32)
    start = pl.multiple_of(LANES * cut.tile(column), LANES)
    own = stage[:, pl.ds(start, window)]

    wait_all(recv, sems.at[1, 0])
    planes[gy] = tree_sum([own] + [recv[k] for k in range(len(plane))])
    for peer in line:
        send(planes.at[gy], planes.at[gy], sems, 2, peer)

    other_lines = lines.at[pl.ds(0, ny - 1)]
    wait_all(other_lines, sems.at[0, 1])
    wait_all(other_lines, sems.at[1, 1])
    old_master, old_moment1, old_moment2 = [
        cut.into(jnp.concatenate([lines[g, k] for g in range(ny)], axis=0), offset) for k in range(3)
    ]

    other_planes = planes.at[pl.ds(0, ny - 1)]
    wait_all(other_planes, sems.at[1, 2])
    summed = tree_sum([planes[g] for g in range(ny)])
    gradient = summed / scale
    new_moment1 = 0.9 * old_moment1 + 0.1 * gradient
    new_moment2 = 0.95 * old_moment2 + 0.05 * gradient * gradient
    first_fix = 1.0 - 0.9**10
    second_fix = 1.0 - 0.95**10
    update = new_moment1 / first_fix / (jnp.sqrt(new_moment2 / second_fix) + 1e-08)
    new_master = old_master - 0.01 * (update + 0.1 * old_master)
    new_params = new_master.astype(jnp.bfloat16)
    shard[...] = new_params
    for _, peer in plane:
        send(shard, gathered.at[column], sems, 3, peer)

    gathered[column] = new_params
    state[0] = new_master
    state[1] = new_moment1
    state[2] = new_moment2
    wait_all(recv, sems.at[0, 0])
    wait_all(other_planes, sems.at[0, 2])
    others = gathered.at[pl.ds(0, len(plane))]
    wait_all(others, sems.at[0, 3])
    wait_all(others, sems.at[1, 3])


def finish(
    sizes, cut, gathered, state, params_out, master_out, moment1_out, moment2_out, params_buf, state_buf, sem
):
    nx, ny, nz = sizes
    rows = state_buf.shape[1]
    gy = lax.axis_index("gy")
    offset = cut.offset(lax.axis_index("gx") * nz + lax.axis_index("gz"))
    copies = []
    for k, out in enumerate((master_out, moment1_out, moment2_out)):
        mine = state[k, 0:rows]
        for g in range(1, ny):
            mine = jnp.where(gy == g, state[k, g * rows : (g + 1) * rows], mine)
        state_buf[k] = cut.out_of(mine, offset)
        copies.append(pltpu.make_async_copy(state_buf.at[k], out, sem.at[k]))
        copies[-1].start()

    lane = lax.broadcasted_iota(jnp.int32, (params_buf.shape[0], LANES), 1)
    for t in range(cut.width // LANES):
        value = None
        for c in range(cut.blocks):
            first = c * cut.own - t * LANES
            if first + cut.own <= 0 or first >= LANES:
                continue
            at = (t - cut.tile(c)) * LANES
            piece = gathered[c, :, at : at + LANES]
            value = piece if value is None else jnp.where(lane >= first, piece, value)
        params_buf[:, t * LANES : (t + 1) * LANES] = value
    copies.append(pltpu.make_async_copy(params_buf, params_out, sem.at[3]))
    copies[-1].start()
    for copy in copies:
        copy.wait()


def solution(mesh):
    sizes = tuple(mesh.shape[axis] for axis in ("gx", "gy", "gz"))
    nx, ny, nz = sizes

    def body(grads, counts, total_tokens, master, moment1, moment2):
        micro, _, all_rows, width = grads.shape[1:]
        rows, own = master.shape[1:]
        cut = Cut(width, nx * nz)
        hbm = pl.BlockSpec(memory_space=pltpu.HBM)
        vmem = pl.BlockSpec(memory_space=pltpu.VMEM)
        scalar = pl.BlockSpec(memory_space=pltpu.SMEM)
        part = jax.ShapeDtypeStruct((rows, own), jnp.float32)
        gathered, state = pl.pallas_call(
            functools.partial(kernel, sizes, cut),
            out_shape=[
                pltpu.VMEM((nx * nz, all_rows, cut.window), jnp.bfloat16),
                pltpu.VMEM((3, all_rows, cut.window), jnp.float32),
            ],
            in_specs=[hbm, scalar, scalar, hbm, hbm, hbm],
            out_specs=[vmem] * 2,
            scratch_shapes=[
                pltpu.VMEM((micro, all_rows, width), jnp.bfloat16),
                pltpu.VMEM((ny, 3, rows, own), jnp.float32),
                pltpu.VMEM((all_rows, width), jnp.float32),
                pltpu.VMEM((nx * nz - 1, all_rows, cut.window), jnp.float32),
                pltpu.VMEM((ny, all_rows, cut.window), jnp.float32),
                pltpu.VMEM((all_rows, cut.window), jnp.bfloat16),
                pltpu.SemaphoreType.DMA((4,)),
                pltpu.SemaphoreType.DMA((2, 4)),
            ],
            compiler_params=pltpu.CompilerParams(collective_id=0, has_side_effects=True),
            name="step",
        )(
            grads.reshape(micro, all_rows, width),
            counts,
            total_tokens,
            master.reshape(rows, own),
            moment1.reshape(rows, own),
            moment2.reshape(rows, own),
        )
        params, *parts = pl.pallas_call(
            functools.partial(finish, sizes, cut),
            out_shape=[jax.ShapeDtypeStruct((all_rows, width), jnp.bfloat16), part, part, part],
            in_specs=[vmem] * 2,
            out_specs=[hbm] * 4,
            scratch_shapes=[
                pltpu.VMEM((all_rows, width), jnp.bfloat16),
                pltpu.VMEM((3, rows, own), jnp.float32),
                pltpu.SemaphoreType.DMA((4,)),
            ],
            name="finish",
        )(
            pltpu.with_memory_space_constraint(gathered, pltpu.VMEM),
            pltpu.with_memory_space_constraint(state, pltpu.VMEM),
        )
        return (params[None], *(array[None] for array in parts))

    sharded = P(None, "gy", ("gx", "gz"))
    return jax.shard_map(
        body,
        mesh=mesh,
        in_specs=(P(("gx", "gy", "gz"), None, None, None, None), P(("gx", "gy", "gz")), P(), sharded, sharded, sharded),
        out_specs=(P(), sharded, sharded, sharded),
        check_vma=False,
    )
```

time: 20.6 us -> 19 us (0.922)
  Pallas kernels: 18.5 us -> 16.9 us
    pallas_call x1, Pallas kernels: 17.7 us -> 16.1 us  [body(): pl.pallas_call(functools.partial(kernel, sizes, cut), out_shape=[pltpu.VM...]
where the time goes in v3:
time: 19 us; the launch traced here: 18.8 us
  Pallas kernels  16.9 us (89%)
  between operations  1.93 us (10%)
    pallas_call x1, Pallas kernels, body(): pl.pallas_call(functools.partial(kernel, sizes, cut), out_shape=[pltpu.VM...  16.1 us
    pallas_call x1, Pallas kernels, body(): pl.pallas_call(functools.partial(finish, sizes, cut), out_shape=[jax.Shap...  0.83 us

profile of v3, /device:TPU:0, one launch (start us, length us, event | category | flops | bytes accessed | tf_op | source)
XLA Modules:
  0.0 18.8 jit_solution(17144038510934039946)
XLA Ops:
  1.9 16.1 %step.1 = (bf16[8,8,512]{2,1,0:T(8,128)(2,1)S(1)}, f32[3,8,512]{2,1,0:T(8,128)S(1)}) custom-call(bf16[4,8,3584]{2,1,0:T(8,128)(2,1)} %bitcast.8, s32[1]{0:T(128)S(6)} %copy.10.counts, s32[1]{0:T(128)S(6)} %copy.11.tokens, f32[2,448]{1,0:T(2,128)} %bitcast.9, f32[2,448]{1,0:T(2,128)} %bitcast.10, f32[2,448]{1,0:T(2,128)} %bitcast.11), custom_call_target="tpu_custom_call" | custom-call | tf_op jit(solution)/shard_map/step/pallas_call | solution.py:235
  18.0 0.8 %finish.1 = (bf16[8,3584]{1,0:T(8,128)(2,1)}, f32[2,448]{1,0:T(2,128)}, f32[2,448]{1,0:T(2,128)}, f32[2,448]{1,0:T(2,128)}) custom-call(bf16[8,8,512]{2,1,0:T(8,128)(2,1)S(1)} %get-tuple-element.10.gathered, f32[3,8,512]{2,1,0:T(8,128)S(1)} %get-tuple-element.11.state), custom_call_target="tpu_custom_call" | custom-call | tf_op jit(solution)/shard_map/finish/pallas_call | solution.py:263
